TPU v7x, 128 devices: a whole 4x4x4 slice. The times are simulated.
128 devices in a mesh: dp: 8 (over x, core), crop: 4 (over y), tensor: 4 (over z).
Axes of the slice: x: 4, y: 4, z: 4, core: 2. Of those that a mesh axis runs over, the one named last changes fastest.
Arguments:
- hidden_a: bfloat16 [2048, 8192], P('crop', 'dp'), as said below
- hidden_b: bfloat16 [2048, 8192], P('crop', 'dp'), as said below
- weight: bfloat16 [8192, 8192], P('dp', 'tensor')
Outputs:
- weight_grad: float32 [8192, 8192], P(('dp', 'crop'), 'tensor')
Inputs may be any that keep to these rules, and one draw needn't show every extreme that they name: `hidden_a`: nonnegative entries. `hidden_b`: nonnegative entries.
All inputs are finite; a program needn't handle non-finite values.
Results may differ from a plain program's by a relative error of at most 0.0015.
Values may be sent and summed in bfloat16 or wider, within the bound.
A program may use at most 128 MiB of HBM per device.

v0:
```python
import jax
import jax.numpy as jnp
from jax import lax
from jax.sharding import PartitionSpec as P

epsilon = 0.0001


def sent_to_all(array, axis):
    peers = lax.axis_size(axis)
    return lax.all_to_all(
        jnp.broadcast_to(array[None], (peers, *array.shape)), axis, 0, 0, tiled=True
    )


def over_copies(array, axis):
    return sent_to_all(array, axis).sum(axis=0)


def body(hidden_a, hidden_b, weight):
    group_size = lax.axis_size(("dp", "crop"))
    data_count = lax.axis_size("dp")
    block_rows = hidden_a.shape[0]
    local_rows = block_rows // data_count
    total_rows = local_rows * group_size
    left_part = jnp.dot(hidden_a, weight, preferred_element_type=jnp.float32)
    right_part = jnp.dot(hidden_b, weight, preferred_element_type=jnp.float32)
    joined = lax.psum_scatter(
        jnp.stack([left_part, right_part], axis=1), "dp", scatter_dimension=0, tiled=True
    ).astype(jnp.bfloat16)
    stacked = jnp.stack([joined[:, 0, :], joined[:, 1, :]]).astype(jnp.float32)
    col_means = over_copies(jnp.sum(stacked, axis=1), ("dp", "crop")) / total_rows
    centered = stacked - col_means[:, None, :]
    spread = over_copies(jnp.sum(centered * centered, axis=1), ("dp", "crop"))
    deviation = jnp.sqrt(spread / (total_rows - 1.0) + epsilon)
    rounded = centered.astype(jnp.bfloat16)
    everyone = lax.all_gather(rounded, ("dp", "crop"), axis=1, tiled=True)
    gram = jnp.einsum("vrf,vbf->vrb", rounded, everyone, preferred_element_type=jnp.float32)
    gram = over_copies(gram, "tensor")
    gram_low = gram.astype(jnp.bfloat16)
    products = jnp.einsum("vrb,vbf->vrf", gram_low, everyone, preferred_element_type=jnp.float32)
    hinge_rate = jnp.where(deviation < 1.0, 25.0 / ((total_rows - 1.0) * deviation), 0.0)[
        :, None, :
    ]
    differ = stacked[0] - stacked[1]
    pull_term = jnp.stack([differ, -differ]) * (50.0 / total_rows)
    cov_scale = 4.0 / (total_rows - 1.0) ** 2
    row_grads = (
        pull_term - hinge_rate * centered + cov_scale * (products - centered * spread[:, None, :])
    )
    row_grads = row_grads.astype(jnp.bfloat16)
    block_grads = lax.all_gather(row_grads, "dp", axis=1, tiled=True)
    across = (((0,), (0,)), ((), ()))
    left_part = lax.dot_general(
        hidden_a, block_grads[0], across, preferred_element_type=jnp.float32
    )
    right_part = lax.dot_general(
        hidden_b, block_grads[1], across, preferred_element_type=jnp.float32
    )
    return lax.psum_scatter(left_part + right_part, "crop", scatter_dimension=0, tiled=True)


def solution(mesh):
    placed = (P("crop", "dp"), P("crop", "dp"), P("dp", "tensor"))
    return jax.shard_map(
        body, mesh=mesh, in_specs=placed, out_specs=P(("dp", "crop"), "tensor"), check_vma=False
    )
```

profile of v0, /device:TPU:1, one launch (start us, length us, event | category | flops | bytes accessed | tf_op | source)
XLA Modules:
  0.0 376.3 jit_solution(18045313686721249146)
XLA Ops:
  6.5 0.0 copy-start
  6.5 0.0 reduce-scatter.3.cloned.1.call-start
  6.5 0.0 copy-start.4
  6.5 5.0 %convolution_bitcast_fusion = f32[512,1,2048]{2,0,1:T(8,128)S(1)} fusion(bf16[512,1024]{1,0:T(8,128)(2,1)} %param.4, bf16[1024,2048]{1,0:T(8,128)(2,1)} %param.5), kind=kOutput, calls=%fused_computation.2 | convolution fusion | flops 2147483648 | bytes 9437184 | tf_op jit(solution)/shard_map/dot_general | solution.py:27
  11.5 0.0 copy-done
  11.5 0.0 copy-done.4
  11.6 2.4 convolution_bitcast_fusion.1
  13.9 3.8 %pad_maximum_fusion = f32[512,2,2048]{2,0,1:T(8,128)} fusion(f32[512,1,2048]{2,0,1:T(8,128)S(1)} %convolution_bitcast_fusion, f32[512,1,2048]{2,0,1:T(8,128)S(1)} %convolution_bitcast_fusion.1), kind=kLoop, calls=%fused_computation | loop fusion | flops 2097152 | bytes 16777216 | tf_op jit(solution)/shard_map/stack | solution.py:29
  17.7 0.0 reduce-scatter.3.cloned.1.call-update
  17.7 0.0 all-gather.3.cloned.1.call-start
  17.8 55.2 %reduce-scatter.3.cloned.1.call-done = f32[64,2,2048]{2,0,1:T(8,128)} async-done(((f32[512,2,2048]{2,0,1:T(8,128)}), f32[64,2,2048]{2,0,1:T(8,128)}) %reduce-scatter.3.cloned.1.call-update) | async-done | bytes 1048592 | tf_op jit(solution)/shard_map/reduce_scatter | solution.py:28
  73.0 1.3 convert_element_type.15
  74.3 0.1 convert_reduce_fusion
  74.4 0.2 broadcast_in_dim.9
  74.7 17.3 %all_to_all.15 = f32[32,2,2048]{2,1,0:T(2,128)S(1)} all-to-all(f32[32,2,2048]{2,1,0:T(2,128)S(1)} %broadcast_in_dim.9), channel_id=1, replica_groups=mesh['dp'=8,'crop'=4,'tensor'=4] {'dp','crop'}, dimensions={0} | all-to-all | bytes 1048576 | tf_op jit(solution)/shard_map/all_to_all | solution.py:11
  92.0 0.2 reduce_sum.46
  92.1 1.0 multiply_reduce_fusion
  93.1 0.0 all-gather.3.cloned.1.call-update
  93.1 1.0 broadcast_in_dim.10
  94.2 4.5 %all-to-all-start.1 = ((f32[32,2,2048]{2,1,0:T(2,128)}), f32[32,2,2048]{2,1,0:T(2,128)S(1)}, u32[]{:S(2)}, u32[]{:S(2)}) async-start(f32[32,2,2048]{2,1,0:T(2,128)} %broadcast_in_dim.10), calls=%async_computation.2 | async-start | bytes 1048576 | tf_op jit(solution)/shard_map/all_to_all | solution.py:11
  98.6 67.9 %all-gather.3.cloned.1.call-done = bf16[2,2048,2048]{2,1,0:T(8,128)(2,1)} async-done(((bf16[2,64,2048]{2,1,0:T(8,128)(2,1)}), bf16[2,2048,2048]{2,1,0:T(8,128)(2,1)}) %all-gather.3.cloned.1.call-update) | async-done | bytes 16777232 | tf_op jit(solution)/shard_map/all_gather | solution.py:37
  166.5 11.1 %fusion.8 = f32[2,64,2048]{2,1,0:T(8,128)S(1)} fusion(bf16[2,64,2048]{2,1,0:T(8,128)(2,1)} %get-tuple-element.8, bf16[2,2048,2048]{2,1,0:T(8,128)(2,1)} %all-gather.3.cloned.1.call-done), kind=kOutput, calls=%fused_computation.25 | convolution fusion | flops 1073741824 | bytes 18350080 | tf_op jit(solution)/shard_map/vrf,vbf->vrb/dot_general | solution.py:38
  177.6 0.0 all-to-all-done.1
  177.6 2.6 broadcast_in_dim.12
  180.2 4.8 %all-to-all-start.2 = ((f32[4,2,64,2048]{3,2,1,0:T(8,128)}), f32[4,2,64,2048]{3,2,1,0:T(8,128)}, u32[]{:S(2)}, u32[]{:S(2)}) async-start(f32[4,2,64,2048]{3,2,1,0:T(8,128)} %broadcast_in_dim.12), calls=%async_computation.3 | async-start | bytes 8388608 | tf_op jit(solution)/shard_map/all_to_all | solution.py:11
  185.0 0.2 all-gather.5.cloned.1.call-start
  185.3 0.1 fusion.6
  185.3 0.9 fusion.7
  186.2 0.2 reduce_sum.48
  186.4 0.0 copy-start.2
  186.5 47.3 %all-to-all-done.2 = f32[4,2,64,2048]{3,2,1,0:T(8,128)} async-done(((f32[4,2,64,2048]{3,2,1,0:T(8,128)}), f32[4,2,64,2048]{3,2,1,0:T(8,128)}, u32[]{:S(2)}, u32[]{:S(2)}) %all-to-all-start.2) | async-done | bytes 4194336 | tf_op jit(solution)/shard_map/all_to_all | solution.py:11
  233.7 2.6 reduce_sum.49
  236.3 0.0 copy-done.2
  236.4 9.8 %fusion.2 = bf16[2,64,2048]{2,1,0:T(8,128)(2,1)} fusion(bf16[2,2048,2048]{2,1,0:T(8,128)(2,1)} %all-gather.3.cloned.1.call-done, f32[1,64,2048]{2,1,0:T(8,128)S(1)} %get-tuple-element.5, f32[1,64,2048]{2,1,0:T(8,128)S(1)} %copy-done.2, f32[2,2048]{1,0:T(2,128)S(1)} %reduce_sum.48, bf16[2,64,2048]{2,1,0:T(8,128)(2,1)S(1)} %reduce_sum.49, ...), kind=kOutput, calls=%fused_computation.7 | convolution fusion | flops 1076887552 | bytes 19447808 | tf_op jit(solution)/shard_map/vrb,vbf->vrf/dot_general | solution.py:41
  246.1 0.0 all-gather.5.cloned.1.call-update
  246.1 0.0 copy-start.3
  246.2 0.0 reduce-scatter.5.cloned.1.call-start
  246.2 30.5 %all-gather.5.cloned.1.call-done = bf16[2,512,2048]{2,1,0:T(8,128)(2,1)} async-done(((bf16[2,64,2048]{2,1,0:T(8,128)(2,1)}), bf16[2,512,2048]{2,1,0:T(8,128)(2,1)}) %all-gather.5.cloned.1.call-update) | async-done | bytes 4194320 | tf_op jit(solution)/shard_map/all_gather | solution.py:52
  276.7 0.0 copy-start.1
  276.7 4.1 %fusion.3 = f32[2048,1024]{1,0:T(8,128)S(1)} fusion(bf16[512,1024]{1,0:T(8,128)(2,1)S(1)} %copy-done, bf16[2,512,2048]{2,1,0:T(8,128)(2,1)} %all-gather.5.cloned.1.call-done), kind=kOutput, calls=%fused_computation.10 | convolution fusion | flops 2147483648 | bytes 11534336 | tf_op jit(solution)/shard_map/dot_general | solution.py:54
  280.8 0.0 copy-done.3
  280.9 0.0 copy-done.1
  280.9 5.8 %add_bitcast_fusion = f32[1024,2048]{0,1:T(8,128)} fusion(f32[2048,1024]{1,0:T(8,128)S(1)} %fusion.3, bf16[512,1024]{1,0:T(8,128)(2,1)S(1)} %copy-done.3, bf16[2,512,2048]{2,1,0:T(8,128)(2,1)S(1)} %copy-done.1), kind=kOutput, calls=%fused_computation.1 | convolution fusion | flops 2149580800 | bytes 19922944 | tf_op jit(solution)/shard_map/dot_general | solution.py:57
  286.7 0.0 reduce-scatter.5.cloned.1.call-update
  286.7 80.2 %reduce-scatter.5.cloned.1.call-done = f32[256,2048]{0,1:T(8,128)} async-done(((f32[1024,2048]{0,1:T(8,128)}), f32[256,2048]{0,1:T(8,128)}) %reduce-scatter.5.cloned.1.call-update) | async-done | bytes 2097168 | tf_op jit(solution)/shard_map/reduce_scatter | solution.py:60
  366.9 2.9 copy.8
  (3 shorter events, 0.1 us)
Async XLA Ops:
  6.5 5.0 %copy-start = (bf16[512,1024]{1,0:T(8,128)(2,1)S(1)}, bf16[512,1024]{1,0:T(8,128)(2,1)}, u32[]{:S(2)}) copy-start(bf16[512,1024]{1,0:T(8,128)(2,1)} %param.3) | copy-start | bytes 3145732
  6.5 66.4 %reduce-scatter.3.cloned.1.call-start = ((), (), s32[]{:S(2)}) async-start(), calls=%async_computation.5 | async-start | bytes 9437184 | tf_op jit(solution)/shard_map/reduce_scatter | solution.py:28
  6.5 5.0 %copy-start.4 = (bf16[1024,2048]{1,0:T(8,128)(2,1)S(1)}, bf16[1024,2048]{1,0:T(8,128)(2,1)}, u32[]{:S(2)}) copy-start(bf16[1024,2048]{1,0:T(8,128)(2,1)} %param.5) | copy-start | bytes 12582916
  17.7 148.7 %all-gather.3.cloned.1.call-start = ((), (), s32[]{:S(2)}) async-start(), calls=%async_computation.6 | async-start | bytes 17301504 | tf_op jit(solution)/shard_map/all_gather | solution.py:37
  94.2 83.5 %all-to-all-start.1 = ((f32[32,2,2048]{2,1,0:T(2,128)}), f32[32,2,2048]{2,1,0:T(2,128)S(1)}, u32[]{:S(2)}, u32[]{:S(2)}) async-start(f32[32,2,2048]{2,1,0:T(2,128)} %broadcast_in_dim.10), calls=%async_computation.2 | async-start | bytes 1048576 | tf_op jit(solution)/shard_map/all_to_all | solution.py:11
  180.2 53.6 %all-to-all-start.2 = ((f32[4,2,64,2048]{3,2,1,0:T(8,128)}), f32[4,2,64,2048]{3,2,1,0:T(8,128)}, u32[]{:S(2)}, u32[]{:S(2)}) async-start(f32[4,2,64,2048]{3,2,1,0:T(8,128)} %broadcast_in_dim.12), calls=%async_computation.3 | async-start | bytes 8388608 | tf_op jit(solution)/shard_map/all_to_all | solution.py:11
  185.0 91.7 %all-gather.5.cloned.1.call-start = ((), (), s32[]{:S(2)}) async-start(), calls=%async_computation.7 | async-start | bytes 4718592 | tf_op jit(solution)/shard_map/all_gather | solution.py:52
  186.4 49.9 %copy-start.2 = (f32[1,64,2048]{2,1,0:T(8,128)S(1)}, f32[1,64,2048]{2,1,0:T(8,128)}, u32[]{:S(2)}) copy-start(f32[1,64,2048]{2,1,0:T(8,128)} %get-tuple-element.6) | copy-start | bytes 1572868
  246.1 34.7 %copy-start.3 = (bf16[512,1024]{1,0:T(8,128)(2,1)S(1)}, bf16[512,1024]{1,0:T(8,128)(2,1)}, u32[]{:S(2)}) copy-start(bf16[512,1024]{1,0:T(8,128)(2,1)} %param.4) | copy-start | bytes 3145732
  246.2 120.7 %reduce-scatter.5.cloned.1.call-start = ((), (), s32[]{:S(2)}) async-start(), calls=%async_computation.8 | async-start | bytes 10485760 | tf_op jit(solution)/shard_map/reduce_scatter | solution.py:60
  276.7 4.2 %copy-start.1 = (bf16[2,512,2048]{2,1,0:T(8,128)(2,1)S(1)}, bf16[2,512,2048]{2,1,0:T(8,128)(2,1)}, u32[]{:S(2)}) copy-start(bf16[2,512,2048]{2,1,0:T(8,128)(2,1)} %all-gather.5.cloned.1.call-done) | copy-start | bytes 12582916
Sparse Core Ops, SparseCore 0:
  17.9 55.0 reduce-scatter.2
  93.2 73.2 all-gather.2
  246.3 30.3 all-gather.4
  286.8 80.0 reduce-scatter.4
where the time goes:
time: 377 us; the launch traced here: 376 us
  waiting for transfers between devices  281 us (75%)
  matrix products  38.2 us (10%)
  blocking collectives  17.3 us (5%)
  between operations  13.3 us (4%)
  other arithmetic  10.1 us (3%)
  starting transfers between devices  9.61 us (3%)
  local copies, waits for them, and re-layouts  6.74 us (2%)
    reduce_scatter x1, waiting for transfers between devices, body(): lax.psum_scatter(left_part + right_part, 'crop', scatter_dimension=0, til...  80.2 us
    all_gather x1, waiting for transfers between devices, body(): everyone = lax.all_gather(rounded, ('dp', 'crop'), axis=1, tiled=True)  67.9 us
    reduce_scatter x1, waiting for transfers between devices, body(): lax.psum_scatter(jnp.stack([left_part, right_part], axis=1), 'dp', scatte...  55.2 us
    all_to_all x2, waiting for transfers between devices, sent_to_all(): lax.all_to_all(jnp.broadcast_to(array[None], (peers, *array.shape)), axis...  47.3 us
    all_gather x1, waiting for transfers between devices, body(): block_grads = lax.all_gather(row_grads, 'dp', axis=1, tiled=True)  30.5 us
    all_to_all x1, blocking collectives, sent_to_all(): lax.all_to_all(jnp.broadcast_to(array[None], (peers, *array.shape)), axis...  17.3 us
    dot_general x1, matrix products, body(): jnp.einsum('vrf,vbf->vrb', rounded, everyone, preferred_element_type=jnp....  11.1 us
    dot_general x1, matrix products, body(): jnp.einsum('vrb,vbf->vrf', gram_low, everyone, preferred_element_type=jnp...  9.76 us
  transfers between devices with their start and end apart: 6, of which 5 were waited for; matrix products, arithmetic and copies ran while one was open for 4% of the time, Pallas kernels for 0%

commit v1 on v0

--- a/solution.py
+++ b/solution.py
@@ -34,7 +34,10 @@
     spread = over_copies(jnp.sum(centered * centered, axis=1), ("dp", "crop"))
     deviation = jnp.sqrt(spread / (total_rows - 1.0) + epsilon)
     rounded = centered.astype(jnp.bfloat16)
-    everyone = lax.all_gather(rounded, ("dp", "crop"), axis=1, tiled=True)
+    everyone = jnp.concatenate(
+        lax.all_to_all(jnp.stack([rounded] * lax.axis_size(("dp", "crop"))), ("dp", "crop"), 0, 0),
+        axis=1,
+    )
     gram = jnp.einsum("vrf,vbf->vrb", rounded, everyone, preferred_element_type=jnp.float32)
     gram = over_copies(gram, "tensor")
     gram_low = gram.astype(jnp.bfloat16)

time: 377 us -> 516 us (1.37)
  blocking collectives: 17.3 us -> 207 us
  waiting for transfers between devices: 281 us -> 215 us
  local copies, waits for them, and re-layouts: 6.74 us -> 23 us
    all_to_all x0 -> x1, blocking collectives: none -> 189 us  [body(): lax.all_to_all(jnp.stack([rounded] * lax.axis_size(('dp', 'crop'))), ('dp...]
    all_gather x1 -> x0, waiting for transfers between devices: 67.9 us -> none  [body(): everyone = lax.all_gather(rounded, ('dp', 'crop'), axis=1, tiled=True)]
    reshape x0 -> x1, local copies, waits for them, and re-layouts: none -> 14.1 us  [body(): jnp.concatenate(lax.all_to_all(jnp.stack([rounded] * lax.axis_size(('dp',...]
  transfers between devices with their start and end apart: 6 -> 5, of which waited for: 5 -> 4; matrix products, arithmetic and copies ran while one was open for 4% -> 5% of each run, Pallas kernels for 0% -> 0%
where the time goes in v1:
time: 516 us
  waiting for transfers between devices  215 us (42%)
  blocking collectives  207 us (40%)
  matrix products  38 us (7%)
  local copies, waits for them, and re-layouts  23 us (4%)
  between operations  13.3 us (3%)
  starting transfers between devices  10.4 us (2%)
  other arithmetic  9.58 us (2%)
    all_to_all x1, blocking collectives, body(): lax.all_to_all(jnp.stack([rounded] * lax.axis_size(('dp', 'crop'))), ('dp...  189 us
    reduce_scatter x1, waiting for transfers between devices, body(): lax.psum_scatter(left_part + right_part, 'crop', scatter_dimension=0, til...  80.2 us
    reduce_scatter x1, waiting for transfers between devices, body(): lax.psum_scatter(jnp.stack([left_part, right_part], axis=1), 'dp', scatte...  55.2 us
    all_to_all x2, waiting for transfers between devices, sent_to_all(): lax.all_to_all(jnp.broadcast_to(array[None], (peers, *array.shape)), axis...  46.9 us
    all_gather x1, waiting for transfers between devices, body(): block_grads = lax.all_gather(row_grads, 'dp', axis=1, tiled=True)  32.5 us
    all_to_all x1, blocking collectives, sent_to_all(): lax.all_to_all(jnp.broadcast_to(array[None], (peers, *array.shape)), axis...  17.3 us
    reshape x1, local copies, waits for them, and re-layouts, body(): jnp.concatenate(lax.all_to_all(jnp.stack([rounded] * lax.axis_size(('dp',...  14.1 us
    dot_general x1, matrix products, body(): jnp.einsum('vrf,vbf->vrb', rounded, everyone, preferred_element_type=jnp....  10.9 us
  transfers between devices with their start and end apart: 5, of which 4 were waited for; matrix products, arithmetic and copies ran while one was open for 5% of the time, Pallas kernels for 0%

profile of v1, /device:TPU:1, one launch (start us, length us, event | category | flops | bytes accessed | tf_op | source)
XLA Modules:
  0.0 515.8 jit_solution(5875874832589333624)
XLA Ops:
  6.5 0.0 copy-start
  6.5 0.0 reduce-scatter.3.cloned.1.call-start
  6.5 0.0 copy-start.3
  6.5 5.0 convolution_bitcast_fusion
  11.5 0.0 copy-done
  11.5 0.0 copy-done.3
  11.6 2.4 convolution_bitcast_fusion.1
  13.9 3.8 pad_maximum_fusion
  17.7 0.0 reduce-scatter.3.cloned.1.call-update
  17.7 55.2 %reduce-scatter.3.cloned.1.call-done = f32[64,2,2048]{2,0,1:T(8,128)} async-done(((f32[512,2,2048]{2,0,1:T(8,128)}), f32[64,2,2048]{2,0,1:T(8,128)}) %reduce-scatter.3.cloned.1.call-update) | async-done | bytes 1048592 | tf_op jit(solution)/shard_map/reduce_scatter | solution.py:28
  73.0 1.3 convert_element_type.19
  74.3 0.1 convert_reduce_fusion
  74.4 0.2 broadcast_in_dim.9
  74.7 17.3 %all_to_all.20 = f32[32,2,2048]{2,1,0:T(2,128)S(1)} all-to-all(f32[32,2,2048]{2,1,0:T(2,128)S(1)} %broadcast_in_dim.9), channel_id=1, replica_groups=mesh['dp'=8,'crop'=4,'tensor'=4] {'dp','crop'}, dimensions={0} | all-to-all | bytes 1048576 | tf_op jit(solution)/shard_map/all_to_all | solution.py:11
  92.0 0.2 reduce_sum.46
  92.1 0.2 multiply_reduce_fusion
  92.3 2.1 stack.17
  94.5 189.3 %all_to_all.21 = bf16[32,2,64,2048]{3,2,1,0:T(8,128)(2,1)} all-to-all(bf16[32,2,64,2048]{3,2,1,0:T(8,128)(2,1)S(1)} %stack.17), channel_id=1, replica_groups=mesh['dp'=8,'crop'=4,'tensor'=4] {'dp','crop'}, dimensions={0} | all-to-all | bytes 33554432 | tf_op jit(solution)/shard_map/all_to_all | solution.py:38
  283.8 1.0 broadcast_in_dim.10
  284.8 5.3 %all-to-all-start.1 = ((f32[32,2,2048]{2,1,0:T(2,128)}), f32[32,2,2048]{2,1,0:T(2,128)}, u32[]{:S(2)}, u32[]{:S(2)}) async-start(f32[32,2,2048]{2,1,0:T(2,128)} %broadcast_in_dim.10), calls=%async_computation.2 | async-start | bytes 1048576 | tf_op jit(solution)/shard_map/all_to_all | solution.py:11
  290.1 14.1 %copy.11 = bf16[2,32,64,2048]{3,2,1,0:T(8,128)(2,1)} copy(bf16[2,32,64,2048]{3,2,0,1:T(8,128)(2,1)} %bitcast.30) | data formatting | bytes 33554432 | tf_op jit(solution)/shard_map/reshape | solution.py:37
  304.2 10.9 %fusion.8 = f32[2,64,2048]{2,1,0:T(8,128)S(1)} fusion(bf16[2,64,2048]{2,1,0:T(8,128)(2,1)S(1)} %get-tuple-element.8, bf16[2,2048,2048]{2,1,0:T(8,128)(2,1)} %bitcast.28), kind=kOutput, calls=%fused_computation.25 | convolution fusion | flops 1073741824 | bytes 18350080 | tf_op jit(solution)/shard_map/vrf,vbf->vrb/dot_general | solution.py:41
  315.2 0.0 all-to-all-done.1
  315.2 2.6 broadcast_in_dim.12
  317.8 4.9 all-to-all-start.3
  322.6 0.2 all-gather.2.cloned.1.call-start
  322.9 0.1 fusion.6
  322.9 0.1 fusion.7
  323.0 1.2 reduce_sum.48
  324.3 46.9 %all-to-all-done.3 = f32[4,2,64,2048]{3,2,1,0:T(8,128)} async-done(((f32[4,2,64,2048]{3,2,1,0:T(8,128)}), f32[4,2,64,2048]{3,2,1,0:T(8,128)}, u32[]{:S(2)}, u32[]{:S(2)}) %all-to-all-start.3) | async-done | bytes 4194336 | tf_op jit(solution)/shard_map/all_to_all | solution.py:11
  371.2 2.6 reduce_sum.49
  373.8 9.8 %fusion.2 = bf16[2,64,2048]{2,1,0:T(8,128)(2,1)} fusion(bf16[2,2048,2048]{2,1,0:T(8,128)(2,1)} %bitcast.29, f32[1,64,2048]{2,1,0:T(8,128)S(1)} %get-tuple-element.5, f32[1,64,2048]{2,1,0:T(8,128)S(1)} %get-tuple-element.6, f32[2,2048]{1,0:T(2,128)S(1)} %reduce_sum.48, bf16[2,64,2048]{2,1,0:T(8,128)(2,1)S(1)} %reduce_sum.49, ...), kind=kOutput, calls=%fused_computation.7 | convolution fusion | flops 1076887552 | bytes 19447808 | tf_op jit(solution)/shard_map/vrb,vbf->vrf/dot_general | solution.py:44
  383.6 0.0 all-gather.2.cloned.1.call-update
  383.6 0.0 copy-start.2
  383.6 0.0 reduce-scatter.5.cloned.1.call-start
  383.7 32.5 %all-gather.2.cloned.1.call-done = bf16[2,512,2048]{2,1,0:T(8,128)(2,1)} async-done(((bf16[2,64,2048]{2,1,0:T(8,128)(2,1)}), bf16[2,512,2048]{2,1,0:T(8,128)(2,1)}) %all-gather.2.cloned.1.call-update) | async-done | bytes 4194320 | tf_op jit(solution)/shard_map/all_gather | solution.py:55
  416.2 0.0 copy-start.1
  416.2 4.1 fusion.3
  420.3 0.0 copy-done.2
  420.4 0.0 copy-done.1
  420.4 5.8 %add_bitcast_fusion = f32[1024,2048]{0,1:T(8,128)} fusion(f32[2048,1024]{1,0:T(8,128)S(1)} %fusion.3, bf16[512,1024]{1,0:T(8,128)(2,1)S(1)} %copy-done.2, bf16[2,512,2048]{2,1,0:T(8,128)(2,1)S(1)} %copy-done.1), kind=kOutput, calls=%fused_computation.1 | convolution fusion | flops 2149580800 | bytes 19922944 | tf_op jit(solution)/shard_map/dot_general | solution.py:60
  426.2 0.0 reduce-scatter.5.cloned.1.call-update
  426.2 80.2 %reduce-scatter.5.cloned.1.call-done = f32[256,2048]{0,1:T(8,128)} async-done(((f32[1024,2048]{0,1:T(8,128)}), f32[256,2048]{0,1:T(8,128)}) %reduce-scatter.5.cloned.1.call-update) | async-done | bytes 2097168 | tf_op jit(solution)/shard_map/reduce_scatter | solution.py:63
  506.4 2.9 copy.12
  (3 shorter events, 0.1 us)
Async XLA Ops:
  6.5 5.0 copy-start
  6.5 66.5 %reduce-scatter.3.cloned.1.call-start = ((), (), s32[]{:S(2)}) async-start(), calls=%async_computation.6 | async-start | bytes 9437184 | tf_op jit(solution)/shard_map/reduce_scatter | solution.py:28
  6.5 5.0 copy-start.3
  284.8 30.4 %all-to-all-start.1 = ((f32[32,2,2048]{2,1,0:T(2,128)}), f32[32,2,2048]{2,1,0:T(2,128)}, u32[]{:S(2)}, u32[]{:S(2)}) async-start(f32[32,2,2048]{2,1,0:T(2,128)} %broadcast_in_dim.10), calls=%async_computation.2 | async-start | bytes 1048576 | tf_op jit(solution)/shard_map/all_to_all | solution.py:11
  317.8 53.5 %all-to-all-start.3 = ((f32[4,2,64,2048]{3,2,1,0:T(8,128)}), f32[4,2,64,2048]{3,2,1,0:T(8,128)}, u32[]{:S(2)}, u32[]{:S(2)}) async-start(f32[4,2,64,2048]{3,2,1,0:T(8,128)} %broadcast_in_dim.12), calls=%async_computation.4 | async-start | bytes 8388608 | tf_op jit(solution)/shard_map/all_to_all | solution.py:11
  322.6 93.6 %all-gather.2.cloned.1.call-start = ((), (), s32[]{:S(2)}) async-start(), calls=%async_computation.7 | async-start | bytes 4718592 | tf_op jit(solution)/shard_map/all_gather | solution.py:55
  383.6 36.7 %copy-start.2 = (bf16[512,1024]{1,0:T(8,128)(2,1)S(1)}, bf16[512,1024]{1,0:T(8,128)(2,1)}, u32[]{:S(2)}) copy-start(bf16[512,1024]{1,0:T(8,128)(2,1)} %param.4) | copy-start | bytes 3145732
  383.6 122.8 %reduce-scatter.5.cloned.1.call-start = ((), (), s32[]{:S(2)}) async-start(), calls=%async_computation.8 | async-start | bytes 10485760 | tf_op jit(solution)/shard_map/reduce_scatter | solution.py:63
  416.2 4.2 copy-start.1
Sparse Core Ops, SparseCore 0:
  17.9 55.0 reduce-scatter.2
  383.7 32.4 all-gather.1
  426.3 80.0 reduce-scatter.4
